TPU v7x, 256 devices: a whole 4x4x8 slice. The times are simulated.
256 devices in a mesh: sector: 16 (over y, x), term: 16 (over z, core).
Axes of the slice: x: 4, y: 4, z: 8, core: 2. Of those that a mesh axis runs over, the one named last changes fastest.
Arguments:
- wavefunction: float32 [16, 256, 256], P('sector'), may hold values from -6 to 6
- left_env: float32 [3072, 256, 256], P(('sector', 'term')), may hold values from -0.02734375 to 0.02734375
- right_env: float32 [3072, 256, 256], P(('sector', 'term')), may hold values from -0.375 to 0.375
- in_sector: int32 [3072], P(('sector', 'term')), may hold values from 0 to 15
- out_sector: int32 [3072], P(('sector', 'term')), may hold values from 0 to 15
- precond: float32 [16, 256, 256], P('sector'), may hold values from 2 to 4
- shifts: float32 [2], replicated, may hold values from 0.2 to 1
Outputs:
- corrected: float32 [16, 256, 256], P('sector')
- residual_norms: float32 [2], replicated
All inputs are finite; a program needn't handle non-finite values.
Results may differ from a plain program's by a relative error of at most 0.0001.
Values sent between devices are 32-bit elements; how exact they have to be, the bound alone decides.
No kernel may reach another device: no remote copies, remote signals or barrier semaphores. Data moves between devices by JAX's collectives and lax.ppermute only.
A program may use at most 64 MiB of HBM per device.

v0:
```python
import jax
import jax.numpy as jnp
from jax import lax
from jax.sharding import Mesh
from jax.sharding import PartitionSpec as P

ITERS = 2
SECTOR = ("sector_0", "sector_1")
SECTOR_TERM = ("sector_0", "sector_1", "term")


def sum_by_axis(value, axes, dim):
    for axis in axes:
        value = lax.psum_scatter(value, axis, scatter_dimension=dim, tiled=True)
    return value


def total_of_pieces(value, axis):
    tiles = lax.all_gather(value, axis)
    return tiles.sum(axis=0)


def by_axis(value, axes):
    for axis in axes:
        value = lax.psum(value, axis)
    return value


def apply_tasks(full, left_env, right_env, in_sector, out_sector):

    def one_task(total, item):
        left, right, source, target = item
        block = lax.dynamic_index_in_dim(full, source, 0, keepdims=False)
        middle = jnp.dot(
            left, block, precision=lax.Precision.HIGHEST, preferred_element_type=jnp.float32
        )
        result = jnp.dot(
            middle, right, precision=lax.Precision.HIGHEST, preferred_element_type=jnp.float32
        )
        current = lax.dynamic_index_in_dim(total, target, 0, keepdims=False)
        total = lax.dynamic_update_index_in_dim(total, current + result, target, 0)
        return (total, None)

    start = jnp.zeros(full.shape, jnp.float32)
    total, _ = lax.scan(one_task, start, (left_env, right_env, in_sector, out_sector))
    return total


def correction(sigma, psi, precond, shift):
    residual = sigma - shift * psi
    updated = psi - residual / (precond - shift)
    return (updated, jnp.sum(residual * residual), jnp.sum(updated * updated))


def per_device(wavefunction, left_env, right_env, in_sector, out_sector, precond, shifts):
    full = lax.all_gather(wavefunction, SECTOR, axis=0, tiled=True)
    norms = []
    psi = wavefunction
    count = lax.axis_size(SECTOR) * psi.size
    for step in range(ITERS):
        partial_value = apply_tasks(full, left_env, right_env, in_sector, out_sector)
        owned = sum_by_axis(partial_value, SECTOR, 0)
        sigma = total_of_pieces(owned, "term")
        updated, res_sq, upd_sq = correction(sigma, psi, precond, shifts[step])
        res_total, upd_total = (by_axis(res_sq, SECTOR), by_axis(upd_sq, SECTOR))
        norms.append(jnp.sqrt(res_total))
        psi = updated / jnp.sqrt(upd_total / count + 1e-06)
        if step + 1 < ITERS:
            full = lax.all_gather(psi, SECTOR, axis=0, tiled=True)
    return (psi, jnp.stack(norms))


def solution(mesh):
    torus = Mesh(mesh.devices.reshape(4, 4, mesh.shape["term"]), ("sector_0", "sector_1", "term"))
    placed = (
        P(SECTOR, None, None),
        P(SECTOR_TERM, None, None),
        P(SECTOR_TERM, None, None),
        P(SECTOR_TERM),
        P(SECTOR_TERM),
        P(SECTOR, None, None),
        P(),
    )
    return jax.shard_map(
        per_device,
        mesh=torus,
        in_specs=placed,
        out_specs=(P(SECTOR, None, None), P()),
        check_vma=False,
    )
```

profile of v0, /device:TPU:32, one launch (start us, length us, event | category | flops | bytes accessed | tf_op | source)
XLA Modules:
  0.0 659.7 jit_solution(3317030970159490162)
XLA Ops:
  8.0 61.5 %all-gather.7.cloned.1.call-done = f32[16,256,256]{2,1,0:T(8,128)} async-done(((f32[1,256,256]{2,1,0:T(8,128)}), f32[16,256,256]{2,1,0:T(8,128)}) %all-gather.7.cloned.1.call-update) | async-done | bytes 4194320 | tf_op jit(solution)/shard_map/all_gather | solution.py:56
  69.5 2.4 broadcast.3.clone
  71.9 114.1 %while.20 = (s32[]{:T(128)}, f32[16,256,256]{2,1,0:T(8,128)}, s32[12]{0:T(128)S(1)}, f32[12,256,256]{2,1,0:T(8,128)}, s32[12]{0:T(128)S(1)}, /*index=5*/f32[16,2...) while((s32[]{:T(128)}, f32[16,256,256]{2,1,0:T(8,128)}, s32[12]{0:T(128)S(1)}, ...), condition=%wide.region_1.2_spmd, body=%wide.region_0.1_spmd.sunk | while | flops 402718720 | bytes 2360525 | solution.py:45
  79.4 2.0 fusion.42
  88.9 2.1 fusion.42
  98.4 2.0 fusion.42
  107.9 2.1 fusion.42
  117.4 2.0 fusion.42
  126.9 2.1 fusion.42
  131.5 1.4 fusion.41
  136.4 2.1 fusion.42
  141.0 1.4 fusion.41
  145.9 2.0 fusion.42
  155.4 2.1 fusion.42
  160.0 1.4 fusion.41
  164.9 2.1 fusion.42
  169.5 1.4 fusion.41
  174.5 2.1 fusion.42
  184.0 2.1 fusion.42
  186.1 49.2 %reduce-scatter.5.cloned.1.call-done = f32[4,256,256]{2,1,0:T(8,128)} async-done(((f32[16,256,256]{2,1,0:T(8,128)}), f32[4,256,256]{2,1,0:T(8,128)}) %reduce-scatter.5.cloned.1.call-update) | async-done | bytes 1048592 | tf_op jit(solution)/shard_map/reduce_scatter | solution.py:14
  235.4 28.5 %reduce-scatter.7.cloned.1.call-done = f32[1,256,256]{2,1,0:T(8,128)} async-done(((f32[4,256,256]{2,1,0:T(8,128)}), f32[1,256,256]{2,1,0:T(8,128)}) %reduce-scatter.7.cloned.1.call-update) | async-done | bytes 262160 | tf_op jit(solution)/shard_map/reduce_scatter | solution.py:14
  264.6 42.5 %all-gather.11.cloned.1.call-done = f32[16,256,256]{2,1,0:T(8,128)} async-done(((f32[1,256,256]{2,1,0:T(8,128)}), f32[16,256,256]{2,1,0:T(8,128)}) %all-gather.11.cloned.1.call-update) | async-done | bytes 4194320 | tf_op jit(solution)/shard_map/all_gather | solution.py:19
  307.1 2.5 reduce.2
  311.0 11.1 %psum.56 = f32[]{:T(128)} all-reduce(f32[]{:T(128)} %get-tuple-element.114), channel_id=1, replica_groups=mesh['sector_0'=4,'sector_1'=4,'term'=16] {'sector_0'}, use_global_device_ids=true, to_apply=%region_6.7 | all-reduce | flops 1 | bytes 8 | tf_op jit(solution)/shard_map/psum | solution.py:25
  322.1 11.0 %psum.57 = f32[]{:T(128)} all-reduce(f32[]{:T(128)} %psum.56), channel_id=1, replica_groups=mesh['sector_0'=4,'sector_1'=4,'term'=16] {'sector_1'}, use_global_device_ids=true, to_apply=%region_7.8 | all-reduce | flops 1 | bytes 8 | tf_op jit(solution)/shard_map/psum | solution.py:25
  334.6 51.1 %all-gather.9.cloned.1.call-done = f32[16,256,256]{2,1,0:T(8,128)} async-done(((f32[1,256,256]{2,1,0:T(8,128)}), f32[16,256,256]{2,1,0:T(8,128)}) %all-gather.9.cloned.1.call-update) | async-done | bytes 4194320 | tf_op jit(solution)/shard_map/all_gather | solution.py:69
  385.7 2.4 broadcast.3
  388.1 114.1 %while.21 = (s32[]{:T(128)}, f32[16,256,256]{2,1,0:T(8,128)}, s32[12]{0:T(128)S(1)}, f32[12,256,256]{2,1,0:T(8,128)}, s32[12]{0:T(128)S(1)}, /*index=5*/f32[16,2...) while((s32[]{:T(128)}, f32[16,256,256]{2,1,0:T(8,128)}, s32[12]{0:T(128)S(1)}, ...), condition=%wide.region_9.10_spmd, body=%wide.region_8.9_spmd.sunk | while | flops 402718720 | bytes 2360525 | solution.py:45
  395.5 2.0 fusion.48
  405.0 2.1 fusion.48
  414.6 2.0 fusion.48
  424.0 2.1 fusion.48
  433.6 2.0 fusion.48
  443.0 2.1 fusion.48
  447.6 1.4 fusion.47
  452.6 2.1 fusion.48
  462.1 2.0 fusion.48
  471.6 2.1 fusion.48
  481.1 2.1 fusion.48
  485.7 1.4 fusion.47
  490.6 2.1 fusion.48
  500.1 2.1 fusion.48
  502.3 49.2 %reduce-scatter.9.cloned.1.call-done = f32[4,256,256]{2,1,0:T(8,128)} async-done(((f32[16,256,256]{2,1,0:T(8,128)}), f32[4,256,256]{2,1,0:T(8,128)}) %reduce-scatter.9.cloned.1.call-update) | async-done | bytes 1048592 | tf_op jit(solution)/shard_map/reduce_scatter | solution.py:14
  551.6 28.5 %reduce-scatter.11.cloned.1.call-done = f32[1,256,256]{2,1,0:T(8,128)} async-done(((f32[4,256,256]{2,1,0:T(8,128)}), f32[1,256,256]{2,1,0:T(8,128)}) %reduce-scatter.11.cloned.1.call-update) | async-done | bytes 262160 | tf_op jit(solution)/shard_map/reduce_scatter | solution.py:14
  580.1 43.3 %all-gather.13.cloned.1.call-done = f32[16,256,256]{2,1,0:T(8,128)} async-done(((f32[1,256,256]{2,1,0:T(8,128)}), f32[16,256,256]{2,1,0:T(8,128)}) %all-gather.13.cloned.1.call-update) | async-done | bytes 4194320 | tf_op jit(solution)/shard_map/all_gather | solution.py:19
  623.4 2.5 reduce.3
  627.3 11.2 %all-reduce.1 = (f32[]{:T(128)}, f32[]{:T(128)}, f32[]{:T(128)}) all-reduce(f32[]{:T(128)} %get-tuple-element.112, f32[]{:T(128)} %get-tuple-element.117, f32[]{:T(128)} %get-tuple-element.116), channel_id=1, replica_groups=mesh['sector_0'=4,'sector_1'=4,'term'=16] {'sector_0'}, use_global_device_ids=true, to_apply=%region_14.15 | all-reduce | flops 3 | bytes 24 | tf_op jit(solution)/shard_map/psum | solution.py:25
  638.4 11.1 %all-reduce = (f32[]{:T(128)}, f32[]{:T(128)}, f32[]{:T(128)}) all-reduce(f32[]{:T(128)} %get-tuple-element.109, f32[]{:T(128)} %get-tuple-element.110, f32[]{:T(128)} %get-tuple-element.111), channel_id=1, replica_groups=mesh['sector_0'=4,'sector_1'=4,'term'=16] {'sector_1'}, use_global_device_ids=true, to_apply=%region_15.16 | all-reduce | flops 3 | bytes 24 | tf_op jit(solution)/shard_map/psum | solution.py:25
  (122 shorter events, 83.5 us)
Async XLA Ops:
  7.2 64.7 %copy-start.4 = (s32[12]{0:T(128)S(1)}, s32[12]{0:T(128)}, u32[]{:S(2)}) copy-start(s32[12]{0:T(128)} %param.14) | copy-start | bytes 148
  7.2 64.7 %copy-start.3 = (s32[12]{0:T(128)S(1)}, s32[12]{0:T(128)}, u32[]{:S(2)}) copy-start(s32[12]{0:T(128)} %param.15) | copy-start | bytes 148
  7.2 62.3 %all-gather.7.cloned.1.call-start = ((), (), s32[]{:S(2)}) async-start(), calls=%async_computation.4 | async-start | bytes 4456448 | tf_op jit(solution)/shard_map/all_gather | solution.py:56
  7.9 227.4 %reduce-scatter.5.cloned.1.call-start = ((), (), s32[]{:S(2)}) async-start(), calls=%async_computation.5 | async-start | bytes 5242880 | tf_op jit(solution)/shard_map/reduce_scatter | solution.py:14
  186.0 78.0 %copy-start.2 = (f32[2]{0:T(128)S(1)}, f32[2]{0:T(128)}, u32[]{:S(2)}) copy-start(f32[2]{0:T(128)} %param.17) | copy-start | bytes 28
  186.0 123.6 %copy-start = (f32[1,256,256]{2,1,0:T(8,128)S(1)}, f32[1,256,256]{2,1,0:T(8,128)}, u32[]{:S(2)}) copy-start(f32[1,256,256]{2,1,0:T(8,128)} %param.11) | copy-start | bytes 786436
  186.0 123.6 %copy-start.1 = (f32[1,256,256]{2,1,0:T(8,128)S(1)}, f32[1,256,256]{2,1,0:T(8,128)}, u32[]{:S(2)}) copy-start(f32[1,256,256]{2,1,0:T(8,128)} %param.16) | copy-start | bytes 786436
  186.1 77.9 %reduce-scatter.7.cloned.1.call-start = ((), (), s32[]{:S(2)}) async-start(), calls=%async_computation.6 | async-start | bytes 1310720 | tf_op jit(solution)/shard_map/reduce_scatter | solution.py:14
  235.4 71.7 %all-gather.11.cloned.1.call-start = ((), (), s32[]{:S(2)}) async-start(), calls=%async_computation.10 | async-start | bytes 4456448 | tf_op jit(solution)/shard_map/all_gather | solution.py:19
  264.0 121.7 %all-gather.9.cloned.1.call-start = ((), (), s32[]{:S(2)}) async-start(), calls=%async_computation.7 | async-start | bytes 4456448 | tf_op jit(solution)/shard_map/all_gather | solution.py:69
  334.6 216.9 %reduce-scatter.9.cloned.1.call-start = ((), (), s32[]{:S(2)}) async-start(), calls=%async_computation.8 | async-start | bytes 5242880 | tf_op jit(solution)/shard_map/reduce_scatter | solution.py:14
  502.2 77.9 %reduce-scatter.11.cloned.1.call-start = ((), (), s32[]{:S(2)}) async-start(), calls=%async_computation.9 | async-start | bytes 1310720 | tf_op jit(solution)/shard_map/reduce_scatter | solution.py:14
  551.5 71.9 %all-gather.13.cloned.1.call-start = ((), (), s32[]{:S(2)}) async-start(), calls=%async_computation.11 | async-start | bytes 4456448 | tf_op jit(solution)/shard_map/all_gather | solution.py:19
Sparse Core Ops, SparseCore 0:
  10.4 59.0 all-gather.6
  186.2 49.1 reduce-scatter.4
  237.9 26.0 reduce-scatter.6
  265.7 41.4 all-gather.10
  334.7 50.9 all-gather.8
  502.3 49.1 reduce-scatter.8
  554.0 26.0 reduce-scatter.10
  581.9 41.4 all-gather.12
where the time goes:
time: 663 us; the launch traced here: 660 us
  waiting for transfers between devices  355 us (54%)
  loops' own time  93.6 us (14%)
  matrix products  83.2 us (13%)
  local copies, waits for them, and re-layouts  56.9 us (9%)
  blocking collectives  44.3 us (7%)
  between operations  16.9 us (3%)
  other arithmetic  9.81 us (1%)
    reduce_scatter x4, waiting for transfers between devices, sum_by_axis(): value = lax.psum_scatter(value, axis, scatter_dimension=dim, tiled=True)  156 us
    another operation x2, loops' own time, apply_tasks(): lax.scan(one_task, start, (left_env, right_env, in_sector, out_sector))  93.6 us
    all_gather x2, waiting for transfers between devices, total_of_pieces(): tiles = lax.all_gather(value, axis)  85.7 us
    all_gather x1, waiting for transfers between devices, per_device(): full = lax.all_gather(wavefunction, SECTOR, axis=0, tiled=True)  61.5 us
    all_gather x1, waiting for transfers between devices, per_device(): full = lax.all_gather(psi, SECTOR, axis=0, tiled=True)  51.1 us
    dot_general x24, matrix products, one_task(): jnp.dot(middle, right, precision=lax.Precision.HIGHEST, preferred_element...  49.3 us
    psum x4, blocking collectives, by_axis(): value = lax.psum(value, axis)  44.3 us
    dot_general x24, matrix products, one_task(): jnp.dot(left, block, precision=lax.Precision.HIGHEST, preferred_element_t...  33.9 us
  transfers between devices with their start and end apart: 8, of which 8 were waited for; matrix products, arithmetic and copies ran while one was open for 0% of the time, Pallas kernels for 0%

commit v1 on v0

v1 whole, which is shorter than its diff:
```python
import jax
import jax.numpy as jnp
from jax import lax
from jax.experimental import pallas as pl
from jax.experimental.pallas import tpu as pltpu
from jax.sharding import Mesh
from jax.sharding import PartitionSpec as P

ITERS = 2
SECTOR = ("sector_0", "sector_1")
SECTOR_TERM = ("sector_0", "sector_1", "term")
EVERY = ("term", "sector_0", "sector_1")


def split(value):
    high = value.astype(jnp.bfloat16)
    return high, (value - high.astype(jnp.float32)).astype(jnp.bfloat16)


def product(left, right):
    left_high, left_low = split(left)
    right_high, right_low = split(right)

    def part(a, b):
        return jnp.dot(a, b, preferred_element_type=jnp.float32)

    return part(left_high, right_high) + (part(left_low, right_high) + part(left_high, right_low))


def task_body(source, target, psi, left, right, total):
    step = pl.program_id(0)

    @pl.when(step == 0)
    def _():
        total[...] = jnp.zeros_like(total)

    total[target[step]] += product(product(left[0], psi[0]), right[0])


def apply_tasks(full, left_env, right_env, in_sector, out_sector):
    tasks, rows, cols = left_env.shape
    block = (1, rows, cols)
    return pl.pallas_call(
        task_body,
        grid_spec=pltpu.PrefetchScalarGridSpec(
            num_scalar_prefetch=2,
            grid=(tasks,),
            in_specs=[
                pl.BlockSpec(block, lambda t, source, target: (source[t], 0, 0)),
                pl.BlockSpec(block, lambda t, source, target: (t, 0, 0)),
                pl.BlockSpec(block, lambda t, source, target: (t, 0, 0)),
            ],
            out_specs=pl.BlockSpec(full.shape, lambda t, source, target: (0, 0, 0)),
        ),
        out_shape=jax.ShapeDtypeStruct(full.shape, jnp.float32),
        compiler_params=pltpu.CompilerParams(
            dimension_semantics=("arbitrary",), vmem_limit_bytes=24 << 20
        ),
        cost_estimate=pl.CostEstimate(
            flops=12 * tasks * rows * rows * cols,
            bytes_accessed=4 * (3 * tasks * rows * cols + full.size),
            transcendentals=0,
        ),
        name="tasks",
    )(in_sector, out_sector, full, left_env, right_env)


def per_device(wavefunction, left_env, right_env, in_sector, out_sector, precond, shifts):
    full = lax.all_gather(wavefunction, SECTOR, axis=0, tiled=True)
    norms = []
    psi = wavefunction
    count = lax.axis_size(SECTOR) * psi.size
    for step in range(ITERS):
        partial_value = apply_tasks(full, left_env, right_env, in_sector, out_sector)
        owned = lax.psum_scatter(partial_value, SECTOR, scatter_dimension=0, tiled=True)
        sigma = lax.all_gather(owned, "term").sum(axis=0)
        shift = shifts[step]
        residual = sigma - shift * psi
        updated = psi - residual / (precond - shift)
        sums = lax.psum(jnp.stack([jnp.sum(residual * residual), jnp.sum(updated * updated)]), SECTOR)
        norms.append(jnp.sqrt(sums[0]))
        psi = updated / jnp.sqrt(sums[1] / count + 1e-06)
        if step + 1 < ITERS:
            full = lax.all_gather(psi, SECTOR, axis=0, tiled=True)
    return (psi, jnp.stack(norms))


def solution(mesh):
    torus = Mesh(mesh.devices.reshape(4, 4, mesh.shape["term"]), ("sector_0", "sector_1", "term"))
    placed = (
        P(SECTOR, None, None),
        P(SECTOR_TERM, None, None),
        P(SECTOR_TERM, None, None),
        P(SECTOR_TERM),
        P(SECTOR_TERM),
        P(SECTOR, None, None),
        P(),
    )
    return jax.shard_map(
        per_device,
        mesh=torus,
        in_specs=placed,
        out_specs=(P(SECTOR, None, None), P()),
        check_vma=False,
    )
```

time: 663 us -> 510 us (0.77)
  loops' own time: 93.6 us -> 0 us
  matrix products: 83.2 us -> 0 us
  local copies, waits for them, and re-layouts: 56.9 us -> 17 us
  blocking collectives: 44.3 us -> 80.6 us
  Pallas kernels: 0 us -> 16.5 us
  waiting for transfers between devices: 355 us -> 364 us
    unnamed x8, waiting for transfers between devices: 0.8 us -> 167 us
    reduce_scatter x4 -> x0, waiting for transfers between devices: 156 us -> none  [sum_by_axis(): value = lax.psum_scatter(value, axis, scatter_dimension=dim, tiled=True)]
    another operation x2 -> x0, loops' own time: 93.6 us -> none  [apply_tasks(): lax.scan(one_task, start, (left_env, right_env, in_sector, out_sector))]
    dot_general x48 -> x0, matrix products: 83.2 us -> none  [the longest x24 49.3 us: one_task(): jnp.dot(middle, right, precision=lax.Precision.HIGHEST, preferred_element...]
    dynamic_slice x72 -> x0, local copies, waits for them, and re-layouts: 51.5 us -> none  [the longest x48 28.1 us: apply_tasks(): lax.scan(one_task, start, (left_env, right_env, in_sector, out_sector))]
    psum x4 -> x2, blocking collectives: 44.3 us -> 80.6 us  [per_device(): lax.psum(jnp.stack([jnp.sum(residual * residual), jnp.sum(updated * updat...]
    pallas_call x0 -> x2, Pallas kernels: none -> 16.5 us  [apply_tasks(): pl.pallas_call(task_body, grid_spec=pltpu.PrefetchScalarGridSpec(num_scal...]
    unnamed x10 -> x28, local copies, waits for them, and re-layouts: 0.02 us -> 15.2 us
  transfers between devices with their start and end apart: 8 -> 6, of which waited for: 8 -> 6; matrix products, arithmetic and copies ran while one was open for 0% -> 0% of each run, Pallas kernels for 0% -> 0%
where the time goes in v1:
time: 510 us; the launch traced here: 509 us
  waiting for transfers between devices  364 us (71%)
  blocking collectives  80.6 us (16%)
  local copies, waits for them, and re-layouts  17 us (3%)
  between operations  16.9 us (3%)
  Pallas kernels  16.5 us (3%)
  other arithmetic  14.1 us (3%)
    unnamed x8, waiting for transfers between devices  167 us
    all_gather x2, waiting for transfers between devices, per_device(): sigma = lax.all_gather(owned, 'term').sum(axis=0)  84.7 us
    psum x2, blocking collectives, per_device(): lax.psum(jnp.stack([jnp.sum(residual * residual), jnp.sum(updated * updat...  80.6 us
    all_gather x1, waiting for transfers between devices, per_device(): full = lax.all_gather(wavefunction, SECTOR, axis=0, tiled=True)  61.5 us
    all_gather x1, waiting for transfers between devices, per_device(): full = lax.all_gather(psi, SECTOR, axis=0, tiled=True)  50.5 us
    pallas_call x2, Pallas kernels, apply_tasks(): pl.pallas_call(task_body, grid_spec=pltpu.PrefetchScalarGridSpec(num_scal...  16.5 us
    unnamed x28, local copies, waits for them, and re-layouts  15.2 us
  transfers between devices with their start and end apart: 6, of which 6 were waited for; matrix products, arithmetic and copies ran while one was open for 0% of the time, Pallas kernels for 0%

profile of v1, /device:TPU:32, one launch (start us, length us, event | category | flops | bytes accessed | tf_op | source)
XLA Modules:
  0.0 509.5 jit_solution(5736220737194053297)
XLA Ops:
  7.2 0.0 all-gather.7.cloned.1.call-start
  7.2 0.7 all-gather.7.cloned.1.call-update
  7.9 0.0 reduce-scatter.7.cloned.1.call-start
  7.9 61.5 %all-gather.7.cloned.1.call-done.psi = f32[16,256,256]{2,1,0:T(8,128)} async-done(((f32[1,256,256]{2,1,0:T(8,128)}), f32[16,256,256]{2,1,0:T(8,128)}) %all-gather.7.cloned.1.call-update) | async-done | bytes 4194320 | tf_op jit(solution)/shard_map/all_gather | solution.py:69
  69.5 1.9 copy-done.2
  71.4 1.9 copy-done.4
  73.2 2.2 copy-done.7
  75.4 0.7 copy-done.8
  76.1 0.7 copy-done.10
  76.7 8.3 %tasks.2 = f32[16,256,256]{2,1,0:T(8,128)S(1)} custom-call(s32[12]{0:T(128)S(1)} %copy-done.8, s32[12]{0:T(128)S(1)} %copy-done.10, f32[16,256,256]{2,1,0:T(8,128)S(1)} %copy-done.7, f32[12,256,256]{2,1,0:T(8,128)S(1)} %copy-done.2, f32[12,256,256]{2,1,0:T(8,128)S(1)} %copy-done.4), custom_call_target="tpu_custom_call" | custom-call | flops 2415919104 | bytes 13631488 | tf_op jit(solution)/shard_map/tasks/pallas_call | solution.py:43
  85.0 0.0 copy-start
  85.0 1.9 copy-done
  87.0 0.0 reduce-scatter.7.cloned.1.call-update
  87.0 0.0 copy-start.3
  87.0 0.0 copy-start.9
  87.0 0.0 copy-start.11
  87.0 0.0 all-gather.11.cloned.1.call-start
  87.1 83.3 %reduce-scatter.7.cloned.1.call-done = f32[1,256,256]{2,1,0:T(8,128)} async-done(((f32[16,256,256]{2,1,0:T(8,128)}), f32[1,256,256]{2,1,0:T(8,128)}) %reduce-scatter.7.cloned.1.call-update) | async-done | bytes 262160
  170.4 0.0 all-gather.11.cloned.1.call-update
  170.4 0.0 all-gather.9.cloned.1.call-start
  170.4 0.0 copy-done.13
  170.4 0.6 fusion.2
  171.0 42.1 %all-gather.11.cloned.1.call-done = f32[16,256,256]{2,1,0:T(8,128)} async-done(((f32[1,256,256]{2,1,0:T(8,128)}), f32[16,256,256]{2,1,0:T(8,128)}) %all-gather.11.cloned.1.call-update) | async-done | bytes 4194320 | tf_op jit(solution)/shard_map/all_gather | solution.py:76
  213.1 3.2 reduce.2
  216.3 2.4 multiply_reduce_fusion.2
  218.7 1.3 pad_maximum_fusion
  220.1 40.3 %psum.14 = f32[2]{0:T(128)S(1)} all-reduce(f32[2]{0:T(128)S(1)} %pad_maximum_fusion), channel_id=1, replica_groups=mesh['sector_0'=4,'sector_1'=4,'term'=16] {'sector_0','sector_1'}, use_global_device_ids=true, to_apply=%region_4.0 | all-reduce | flops 2 | bytes 16 | tf_op jit(solution)/shard_map/psum | solution.py:80
  260.4 0.6 fusion
  261.6 0.7 broadcast_divide_fusion.1
  262.4 0.0 all-gather.9.cloned.1.call-update
  262.4 0.0 reduce-scatter.9.cloned.1.call-start
  262.4 50.5 %all-gather.9.cloned.1.call-done.psi = f32[16,256,256]{2,1,0:T(8,128)} async-done(((f32[1,256,256]{2,1,0:T(8,128)}), f32[16,256,256]{2,1,0:T(8,128)}) %all-gather.9.cloned.1.call-update) | async-done | bytes 4194320 | tf_op jit(solution)/shard_map/all_gather | solution.py:84
  312.9 1.9 copy-done.5
  314.8 2.2 copy-done.6
  317.0 8.3 %tasks.3 = f32[16,256,256]{2,1,0:T(8,128)S(1)} custom-call(s32[12]{0:T(128)S(1)} %copy-done.9, s32[12]{0:T(128)S(1)} %copy-done.11, f32[16,256,256]{2,1,0:T(8,128)S(1)} %copy-done.6, f32[12,256,256]{2,1,0:T(8,128)S(1)} %copy-done.3, f32[12,256,256]{2,1,0:T(8,128)S(1)} %copy-done.5), custom_call_target="tpu_custom_call" | custom-call | flops 2415919104 | bytes 13631488 | tf_op jit(solution)/shard_map/tasks/pallas_call | solution.py:43
  325.3 1.9 copy-done.1
  327.2 0.0 reduce-scatter.9.cloned.1.call-update
  327.2 0.0 all-gather.13.cloned.1.call-start
  327.3 83.3 %reduce-scatter.9.cloned.1.call-done = f32[1,256,256]{2,1,0:T(8,128)} async-done(((f32[16,256,256]{2,1,0:T(8,128)}), f32[1,256,256]{2,1,0:T(8,128)}) %reduce-scatter.9.cloned.1.call-update) | async-done | bytes 262160
  410.6 0.0 all-gather.13.cloned.1.call-update
  410.7 42.6 %all-gather.13.cloned.1.call-done = f32[16,256,256]{2,1,0:T(8,128)} async-done(((f32[1,256,256]{2,1,0:T(8,128)}), f32[16,256,256]{2,1,0:T(8,128)}) %all-gather.13.cloned.1.call-update) | async-done | bytes 4194320 | tf_op jit(solution)/shard_map/all_gather | solution.py:76
  453.2 2.5 reduce.3
  455.7 1.4 multiply_reduce_fusion
  457.1 1.3 pad_maximum_fusion.1
  459.0 40.3 %psum.15 = f32[2]{0:T(128)S(1)} all-reduce(f32[2]{0:T(128)S(1)} %pad_maximum_fusion.1), channel_id=1, replica_groups=mesh['sector_0'=4,'sector_1'=4,'term'=16] {'sector_0','sector_1'}, use_global_device_ids=true, to_apply=%region_9.0 | all-reduce | flops 2 | bytes 16 | tf_op jit(solution)/shard_map/psum | solution.py:80
  499.3 0.6 fusion.1
  501.3 0.6 pad_maximum_fusion.2
  501.9 0.7 broadcast_divide_fusion
  (14 shorter events, 0.0 us)
Async XLA Ops:
  7.2 62.3 %all-gather.7.cloned.1.call-start = ((), (), s32[]{:S(2)}) async-start(), calls=%async_computation.2 | async-start | bytes 4456448 | tf_op jit(solution)/shard_map/all_gather | solution.py:69
  7.9 162.5 %reduce-scatter.7.cloned.1.call-start = ((), (), s32[]{:S(2)}) async-start(), calls=%async_computation.6 | async-start | bytes 4456448
  69.5 1.9 copy-start.2
  71.4 1.9 copy-start.4
  73.2 2.2 copy-start.7
  75.4 0.7 copy-start.8
  76.1 0.7 copy-start.10
  85.0 1.9 copy-start
  87.0 83.5 %copy-start.13 = (f32[2]{0:T(128)S(1)}, f32[2]{0:T(128)}, u32[]{:S(2)}) copy-start(f32[2]{0:T(128)} %param.13) | copy-start | bytes 28
  87.0 225.9 %copy-start.3 = (f32[12,256,256]{2,1,0:T(8,128)S(1)}, f32[12,256,256]{2,1,0:T(8,128)}, u32[]{:S(2)}) copy-start(f32[12,256,256]{2,1,0:T(8,128)} %left.3) | copy-start | bytes 9437188
  87.0 225.9 %copy-start.9 = (s32[12]{0:T(128)S(1)}, s32[12]{0:T(128)}, u32[]{:S(2)}) copy-start(s32[12]{0:T(128)} %source.3) | copy-start | bytes 148
  87.0 225.9 %copy-start.11 = (s32[12]{0:T(128)S(1)}, s32[12]{0:T(128)}, u32[]{:S(2)}) copy-start(s32[12]{0:T(128)} %target.3) | copy-start | bytes 148
  87.0 126.1 %all-gather.11.cloned.1.call-start = ((), (), s32[]{:S(2)}) async-start(), calls=%async_computation.4 | async-start | bytes 4456448 | tf_op jit(solution)/shard_map/all_gather | solution.py:76
  170.4 142.5 %all-gather.9.cloned.1.call-start = ((), (), s32[]{:S(2)}) async-start(), calls=%async_computation.3 | async-start | bytes 4456448 | tf_op jit(solution)/shard_map/all_gather | solution.py:84
  262.4 148.2 %reduce-scatter.9.cloned.1.call-start = ((), (), s32[]{:S(2)}) async-start(), calls=%async_computation.7 | async-start | bytes 4456448
  312.9 1.9 copy-start.5
  314.8 2.2 copy-start.6
  325.3 1.9 copy-start.1
  327.2 128.5 %copy-start.12 = (f32[1,256,256]{2,1,0:T(8,128)S(1)}, f32[1,256,256]{2,1,0:T(8,128)}, u32[]{:S(2)}) copy-start(f32[1,256,256]{2,1,0:T(8,128)} %param.12) | copy-start | bytes 786436
  327.2 126.0 %all-gather.13.cloned.1.call-start = ((), (), s32[]{:S(2)}) async-start(), calls=%async_computation.5 | async-start | bytes 4456448 | tf_op jit(solution)/shard_map/all_gather | solution.py:76
Sparse Core Ops, SparseCore 0:
  10.4 59.0 all-gather.6
  87.1 83.1 reduce-scatter.6
  172.2 40.9 all-gather.10
  262.5 50.3 all-gather.8
  327.4 83.2 reduce-scatter.8
  412.3 40.8 all-gather.12
